TPU v7x, 32 devices: a whole 2x2x4 slice. The times are simulated.
32 devices in a mesh: row: 16 (over z, y, core), col: 2 (over x).
Axes of the slice: x: 2, y: 2, z: 4, core: 2. Of those that a mesh axis runs over, the one named last changes fastest.
Arguments:
- positions: float32 [3, 8192], P(None, ('row', 'col')), as said below
- velocities: float32 [3, 8192], P(None, ('row', 'col')), may hold values from -6 to 6
- old_forces: float32 [3, 8192], P(None, ('row', 'col')), may hold values from -6 to 6
- charges: float32 [8192], P(('row', 'col')), may hold values from -3 to 3
- atom_types: int32 [8192], P(('row', 'col')), may hold values from 0 to 7
- type_table: float32 [7, 8], replicated, may hold values from 0.003 to 2, as said below
- tile_pairs: int32 [16, 2, 2, 32], P('row', 'col'), may hold values from -1 to 31, as said below
Outputs:
- new_positions: float32 [3, 8192], P(None, ('row', 'col'))
- new_velocities: float32 [3, 8192], P(None, ('row', 'col'))
- new_forces: float32 [3, 8192], P(None, ('row', 'col'))
Inputs may be any that keep to these rules, and one draw needn't show every extreme that they name: `positions`: the atoms of one block lie together in a cube of its own; the blocks' cubes fill a cubic lattice in the order of the block numbers, at about 0.1 atoms per cubic angstrom. `tile_pairs`: on each device the first n slots hold distinct pairs (a, g) with a below 4 and g below 32, each a tile whose blocks' cubes lie within 12 angstrom of each other; the other slots hold -1 in both entries. n is at most 32, differs from device to device, and equals 32 on the device with the most such tiles when it has 32 or more; the list is a sampled part of each device's near tiles, not all of them. `type_table`: Rows: intrinsic radii 1 to 2, screening scales 0.15 to 0.6, neck weights 0.003 to 0.012, alpha 0.6 to 1, beta 0.3 to 0.9, gamma 0.2 to 0.6, masses 0.5 to 2.
All inputs are finite; a program needn't handle non-finite values.
Results may differ from a plain program's by a relative error of at most 0.0003.
Values sent between devices are 32-bit elements; how exact they have to be, the bound alone decides.
A program may use at most 64 MiB of HBM per device.

v0:
```python
import jax
import jax.numpy as jnp
from jax import lax
from jax.sharding import PartitionSpec as P

TILE = 128
BLK_DEV = 2
GROUP = 4
CUTOFF = 12.0
COULOMB = 32.0
TIMESTEP = 0.5
OFFSET = 0.09
NECK_GAP = 0.5
NECK_WIDTH = 16.0


def taper(dist_sq):
    taper_base = jnp.maximum(1.0 - dist_sq / (CUTOFF * CUTOFF), 0.0)
    return (taper_base * taper_base, -2.0 * taper_base / (CUTOFF * CUTOFF))


def screening(dist_sq, intrinsic, other_radius, other_scale, other_neck):
    soft_sq = dist_sq + intrinsic * intrinsic
    neck_gap = intrinsic + other_radius + NECK_GAP
    neck_off = dist_sq - neck_gap * neck_gap
    neck_bump = jnp.exp(-neck_off * neck_off / NECK_WIDTH)
    volume = other_scale * other_radius * other_radius * other_radius
    descreen = volume / (soft_sq * soft_sq) + other_neck * neck_bump
    slope = -2.0 * volume / (soft_sq * soft_sq * soft_sq) - other_neck * neck_bump * neck_off * (
        2.0 / NECK_WIDTH
    )
    weight, w_slope = taper(dist_sq)
    return (weight * descreen, w_slope * descreen + weight * slope)


def separation(coords_i, coords_j):
    offset_vec = coords_i[:, :, :, None] - coords_j[:, :, None, :]
    return (offset_vec, jnp.sum(offset_vec * offset_vec, axis=1))


def born_terms(side_i, side_j, mask):
    offset_vec, dist_sq = separation(side_i[:, 0:3], side_j[:, 0:3])
    value, slope = screening(
        dist_sq,
        side_i[:, 4][:, :, None],
        side_j[:, 4][:, None, :],
        side_j[:, 5][:, None, :],
        side_j[:, 6][:, None, :],
    )
    return jnp.sum(mask * value, axis=2)[:, None, :]


def pair_terms(side_i, side_j, mask):
    offset_vec, dist_sq = separation(side_i[:, 0:3], side_j[:, 0:3])
    charge_pair = side_i[:, 3][:, :, None] * side_j[:, 3][:, None, :]
    radius_j = side_j[:, -1][:, None, :]
    radii_prod = side_i[:, -1][:, :, None] * radius_j
    radii_exp = jnp.exp(-dist_sq / (4.0 * radii_prod))
    inv_eff = 1.0 / jnp.sqrt(dist_sq + radii_prod * radii_exp)
    inv_cube = inv_eff * inv_eff * inv_eff
    weight, w_slope = taper(dist_sq)
    d_dist = (
        mask
        * charge_pair
        * (w_slope * inv_eff - 0.5 * weight * (1.0 - 0.25 * radii_exp) * inv_cube)
    )
    d_radius = (
        mask
        * -0.5
        * weight
        * charge_pair
        * inv_cube
        * radii_exp
        * (1.0 + dist_sq / (4.0 * radii_prod))
        * radius_j
    )
    direct = 2.0 * COULOMB * jnp.sum(d_dist[:, None] * offset_vec, axis=3)
    return jnp.concatenate([direct, jnp.sum(d_radius, axis=2)[:, None, :]], axis=1)


def chain_terms(side_i, side_j, mask):
    offset_vec, dist_sq = separation(side_i[:, 0:3], side_j[:, 0:3])
    value_ij, slope_ij = screening(
        dist_sq,
        side_i[:, 4][:, :, None],
        side_j[:, 4][:, None, :],
        side_j[:, 5][:, None, :],
        side_j[:, 6][:, None, :],
    )
    value_ji, slope_ji = screening(
        dist_sq,
        side_j[:, 4][:, None, :],
        side_i[:, 4][:, :, None],
        side_i[:, 5][:, :, None],
        side_i[:, 6][:, :, None],
    )
    factor = mask * (side_i[:, -1][:, :, None] * slope_ij + side_j[:, -1][:, None, :] * slope_ji)
    return -2.0 * jnp.sum(factor[:, None] * offset_vec, axis=3)


def radius_terms(born_sum, intrinsic, coef_alpha, coef_beta, coef_gamma):
    scaled = intrinsic * born_sum
    poly_arg = (
        coef_alpha * scaled - coef_beta * scaled * scaled + coef_gamma * scaled * scaled * scaled
    )
    squash = jnp.tanh(poly_arg)
    radius = 1.0 / (1.0 / intrinsic - squash / (intrinsic + OFFSET))
    poly_slope = coef_alpha - 2.0 * coef_beta * scaled + 3.0 * coef_gamma * scaled * scaled
    radius_rate = (
        radius * radius * (1.0 - squash * squash) * poly_slope * intrinsic / (intrinsic + OFFSET)
    )
    return (radius, radius_rate)


def run_tiles(func, rows, pack_i, pack_j, tiles_i, tiles_j, live_f, self_pair, group_count):
    block_total = pack_i.shape[1]
    diagonal = jnp.eye(TILE, dtype=jnp.float32)
    block_ids = jnp.arange(block_total, dtype=jnp.int32)

    def one_turn(turn_index, summed):
        first = turn_index * GROUP
        group_i = lax.dynamic_slice_in_dim(tiles_i, first, GROUP)
        group_j = lax.dynamic_slice_in_dim(tiles_j, first, GROUP)
        group_live = lax.dynamic_slice_in_dim(live_f, first, GROUP)
        group_self = lax.dynamic_slice_in_dim(self_pair, first, GROUP)
        side_i = jnp.moveaxis(jnp.take(pack_i, group_i, axis=1), 1, 0)
        side_j = jnp.moveaxis(jnp.take(pack_j, group_j, axis=1), 1, 0)
        mask = group_live[:, None, None] * (1.0 - group_self[:, None, None] * diagonal)
        partial_sums = func(side_i, side_j, mask)
        owner = (group_i[:, None] == block_ids[None, :]).astype(jnp.float32)
        return summed + jnp.einsum(
            "gk,gra->kra", owner, partial_sums, precision=lax.Precision.HIGHEST
        )

    summed = lax.fori_loop(
        0, group_count, one_turn, jnp.zeros((block_total, rows, TILE), jnp.float32)
    )
    return jnp.moveaxis(summed, 1, 0).reshape(rows, block_total * TILE)


def body(positions, velocities, old_forces, charges, atom_types, type_table, tile_pairs):
    col_count = lax.axis_size("col")
    row_count = lax.axis_size("row")
    col_index = lax.axis_index("col")
    row_index = lax.axis_index("row")
    own_count = positions.shape[1]
    type_ids = jnp.arange(type_table.shape[1], dtype=jnp.int32)
    onehot = (atom_types[None, :] == type_ids[:, None]).astype(jnp.float32)
    params = jnp.sum(type_table[:, :, None] * onehot[None, :, :], axis=1)
    atom_mass = params[6]
    new_positions = (
        positions + TIMESTEP * velocities + TIMESTEP * TIMESTEP / (2.0 * atom_mass) * old_forces
    )
    own_data = jnp.concatenate([new_positions, charges[None, :], params[0:6]], axis=0)
    side_i = lax.all_gather(own_data, "col", axis=1, tiled=True)
    side_j = lax.all_gather(own_data[0:7], "row", axis=1, tiled=True)
    blocks_i = col_count * BLK_DEV
    blocks_j = row_count * BLK_DEV
    pack_i = side_i.reshape(10, blocks_i, TILE)
    pack_j = side_j.reshape(7, blocks_j, TILE)
    tile_list = tile_pairs[0, 0]
    live_slot = tile_list[0] >= 0
    tiles_i = jnp.maximum(tile_list[0], 0)
    tiles_j = jnp.maximum(tile_list[1], 0)
    global_i = row_index * blocks_i + tiles_i
    global_j = (tiles_j // BLK_DEV * col_count + col_index) * BLK_DEV + tiles_j % BLK_DEV
    self_pair = (global_i == global_j).astype(jnp.float32)
    live_f = live_slot.astype(jnp.float32)
    group_count = (jnp.sum(live_slot.astype(jnp.int32)) + GROUP - 1) // GROUP

    def tile_sweep(func, rows, data_i, data_j):
        return run_tiles(
            func, rows, data_i, data_j, tiles_i, tiles_j, live_f, self_pair, group_count
        )

    born_part = tile_sweep(born_terms, 1, pack_i, pack_j)[0]
    born_all = lax.psum(born_part, "col")
    radius_i, rate_i = radius_terms(born_all, side_i[4], side_i[7], side_i[8], side_i[9])
    radius_own = lax.dynamic_slice_in_dim(radius_i, col_index * own_count, own_count)
    radius_j = lax.all_gather(radius_own, "row", axis=0, tiled=True)
    with_radius_i = jnp.concatenate([pack_i, radius_i.reshape(1, blocks_i, TILE)], axis=0)
    with_radius_j = jnp.concatenate([pack_j, radius_j.reshape(1, blocks_j, TILE)], axis=0)
    pair_part = tile_sweep(pair_terms, 4, with_radius_i, with_radius_j)
    grad_all = lax.psum(pair_part[3], "col")
    chain_i = (
        COULOMB * side_i[3] * side_i[3] / (2.0 * radius_i * radius_i) - COULOMB * grad_all
    ) * rate_i
    chain_own = lax.dynamic_slice_in_dim(chain_i, col_index * own_count, own_count)
    chain_j = lax.all_gather(chain_own, "row", axis=0, tiled=True)
    with_chain_i = jnp.concatenate([pack_i, chain_i.reshape(1, blocks_i, TILE)], axis=0)
    with_chain_j = jnp.concatenate([pack_j, chain_j.reshape(1, blocks_j, TILE)], axis=0)
    chain_part = tile_sweep(chain_terms, 3, with_chain_i, with_chain_j)
    force_sum = pair_part[0:3] + chain_part
    new_forces = lax.psum_scatter(force_sum, "col", scatter_dimension=1, tiled=True)
    new_velocities = velocities + TIMESTEP / (2.0 * atom_mass) * (old_forces + new_forces)
    return (new_positions, new_velocities, new_forces)


def solution(mesh):
    return jax.shard_map(
        body,
        mesh=mesh,
        in_specs=(
            P(None, ("row", "col")),
            P(None, ("row", "col")),
            P(None, ("row", "col")),
            P(("row", "col")),
            P(("row", "col")),
            P(),
            P("row", "col", None, None),
        ),
        out_specs=(P(None, ("row", "col")), P(None, ("row", "col")), P(None, ("row", "col"))),
        check_vma=False,
    )
```

profile of v0, /device:TPU:0, one launch (start us, length us, event | category | flops | bytes accessed | tf_op | source)
XLA Modules:
  0.0 163.2 jit_solution(18386366832432704033)
XLA Ops:
  7.2 1.4 maximum_bitcast_fusion
  9.3 0.7 copy-done.8
  9.9 0.7 copy-done.5
  10.8 0.6 copy-done.2
  11.4 0.7 copy-done.9
  12.1 5.3 %all_gather.12 = f32[10,512]{1,0:T(8,128)S(1)} all-gather(f32[10,256]{1,0:T(8,128)S(1)} %pad_maximum_fusion.4), channel_id=1, replica_groups=mesh['row'=16,'col'=2] {'col'}, dimensions={1}, use_global_device_ids=true | all-gather | bytes 30720 | tf_op jit(solution)/shard_map/all_gather | solution.py:155
  17.5 0.7 copy-done.7
  18.2 0.7 slice-done
  18.9 22.5 %all_gather.13 = f32[7,4096]{1,0:T(8,128)S(1)} all-gather(f32[7,256]{1,0:T(8,128)S(1)} %slice-done), channel_id=1, replica_groups=mesh['row'=16,'col'=2] {'row'}, dimensions={1}, use_global_device_ids=true | all-gather | bytes 121856 | tf_op jit(solution)/shard_map/all_gather | solution.py:156
  41.5 2.5 %while.37 = (s32[]{:T(128)}, f32[4,1,128]{2,0,1:T(4,128)S(1)}, s32[]{:T(128)}, s32[32]{0:T(128)S(1)}, f32[32]{0:T(128)S(1)}, /*index=5*/f32[32]{0:T(128)S(1)}, f...) while((s32[]{:T(128)}, f32[4,1,128]{2,0,1:T(4,128)S(1)}, ...), condition=%wide.region_5.6_spmd.clone, body=%wide.region_2.5_spmd.clone.sunk | while | flops 2036306 | bytes 881111 | solution.py:135
  41.6 0.6 gather_fusion.1
  42.2 0.6 gather_fusion
  43.4 0.4 fusion.112
  44.0 11.9 %psum.14 = f32[512]{0:T(512)S(1)} all-reduce(f32[512]{0:T(512)S(1)} %bitcast.173), channel_id=1, replica_groups=mesh['row'=16,'col'=2] {'col'}, use_global_device_ids=true, to_apply=%region_6.7 | all-reduce | flops 512 | bytes 4096 | tf_op jit(solution)/shard_map/psum | solution.py:177
  55.9 22.3 %all-gather = f32[16,1,256]{2,1,0:T(1,128)S(1)} all-gather(f32[1,1,256]{2,1,0:T(1,128)S(1)} %bitcast.177), channel_id=1, replica_groups=mesh['row'=16,'col'=2] {'row'}, dimensions={0}, use_global_device_ids=true | all-gather | bytes 17408 | tf_op jit(solution)/shard_map/all_gather | solution.py:180
  78.4 3.1 %while.38 = (s32[]{:T(128)}, f32[4,4,128]{2,0,1:T(4,128)S(1)}, s32[]{:T(128)}, s32[32]{0:T(128)S(1)}, f32[32]{0:T(128)S(1)}, /*index=5*/f32[32]{0:T(128)S(1)}, f...) while((s32[]{:T(128)}, f32[4,4,128]{2,0,1:T(4,128)S(1)}, ...), condition=%wide.region_11.14_spmd.clone, body=%wide.region_7.13_spmd.clone.sunk | while | flops 3619922 | bytes 1462743 | solution.py:135
  78.5 0.6 gather_fusion.3
  79.1 0.6 gather_fusion.2
  79.8 0.3 fusion.116
  80.2 0.5 fusion.120
  80.8 0.5 fusion.121
  81.5 12.4 %psum.15 = f32[512]{0:T(512)S(1)} all-reduce(f32[512]{0:T(512)S(1)} %slice_bitcast_fusion), channel_id=1, replica_groups=mesh['row'=16,'col'=2] {'col'}, use_global_device_ids=true, to_apply=%region_12.15 | all-reduce | flops 512 | bytes 4096 | tf_op jit(solution)/shard_map/psum | solution.py:184
  94.0 26.8 %all-gather.1 = f32[16,1,256]{2,1,0:T(1,128)S(1)} all-gather(f32[1,1,256]{2,1,0:T(1,128)S(1)} %bitcast.176), channel_id=1, replica_groups=mesh['row'=16,'col'=2] {'row'}, dimensions={0}, use_global_device_ids=true | all-gather | bytes 17408 | tf_op jit(solution)/shard_map/all_gather | solution.py:189
  120.9 3.2 %while.39 = (s32[]{:T(128)}, f32[4,3,128]{2,0,1:T(4,128)S(1)}, s32[]{:T(128)}, s32[32]{0:T(128)S(1)}, f32[32]{0:T(128)S(1)}, /*index=5*/f32[32]{0:T(128)S(1)}, f...) while((s32[]{:T(128)}, f32[4,3,128]{2,0,1:T(4,128)S(1)}, ...), condition=%wide.region_16.19_spmd.clone, body=%wide.region_13.18_spmd.clone.sunk | while | flops 4188242 | bytes 1489367 | solution.py:135
  121.0 0.6 gather_fusion.5
  121.7 0.6 gather_fusion.4
  122.8 0.6 fusion.127
  123.4 0.5 fusion.128
  124.1 0.9 copy.51
  125.0 29.8 %reduce-scatter.4.cloned.1.call-done = f32[256,3]{1,0:T(8,128)} async-done(((f32[512,3]{1,0:T(8,128)}), f32[256,3]{1,0:T(8,128)}) %reduce-scatter.4.cloned.1.call-update) | async-done | bytes 3088
  154.8 1.0 copy.50
  155.7 0.6 multiply_add_fusion
  (90 shorter events, 3.1 us)
Async XLA Ops:
  7.2 147.6 %reduce-scatter.4.cloned.1.call-start = ((), (), s32[]{:S(2)}) async-start(), calls=%async_computation.1 | async-start | bytes 393216
  9.3 0.7 copy-start.8
  9.9 0.7 copy-start.5
  10.6 0.7 copy-start.2
  10.6 0.7 copy-start.6
  10.7 0.7 copy-start.1
  11.4 0.7 copy-start.4
  11.4 0.7 copy-start.9
  12.1 5.3 %copy-start = (f32[10,256]{1,0:T(8,128)}, f32[10,256]{1,0:T(8,128)S(1)}, u32[]{:S(2)}) copy-start(f32[10,256]{1,0:T(8,128)S(1)} %pad_maximum_fusion.4) | copy-start | bytes 30724
  17.5 0.7 copy-start.7
  18.2 0.7 slice-start
  155.7 0.6 copy-start.3
Sparse Core Ops, SparseCore 0:
  125.1 29.6 reduce-scatter.3
where the time goes:
time: 164 us; the launch traced here: 163 us
  blocking collectives  101 us (62%)
  waiting for transfers between devices  29.8 us (18%)
  between operations  14.9 us (9%)
  local copies, waits for them, and re-layouts  9.93 us (6%)
  other arithmetic  6.46 us (4%)
    unnamed x2, waiting for transfers between devices  29.8 us
    all_gather x1, blocking collectives, body(): chain_j = lax.all_gather(chain_own, 'row', axis=0, tiled=True)  26.8 us
    all_gather x1, blocking collectives, body(): side_j = lax.all_gather(own_data[0:7], 'row', axis=1, tiled=True)  22.5 us
    all_gather x1, blocking collectives, body(): radius_j = lax.all_gather(radius_own, 'row', axis=0, tiled=True)  22.3 us
    psum x1, blocking collectives, body(): grad_all = lax.psum(pair_part[3], 'col')  12.4 us
    psum x1, blocking collectives, body(): born_all = lax.psum(born_part, 'col')  11.9 us
    all_gather x1, blocking collectives, body(): side_i = lax.all_gather(own_data, 'col', axis=1, tiled=True)  5.34 us
    unnamed x25, local copies, waits for them, and re-layouts  5.24 us
  transfers between devices with their start and end apart: 1, of which 1 were waited for; matrix products, arithmetic and copies ran while one was open for 0% of the time, Pallas kernels for 0%

commit v1 on v0

--- a/solution.py
+++ b/solution.py
@@ -153,7 +153,9 @@
     )
     own_data = jnp.concatenate([new_positions, charges[None, :], params[0:6]], axis=0)
     side_i = lax.all_gather(own_data, "col", axis=1, tiled=True)
-    side_j = lax.all_gather(own_data[0:7], "row", axis=1, tiled=True)
+    my_data = own_data[0:7]
+    now = lax.all_gather(my_data, "row")
+    side_j = jnp.concatenate(now, axis=1)
     blocks_i = col_count * BLK_DEV
     blocks_j = row_count * BLK_DEV
     pack_i = side_i.reshape(10, blocks_i, TILE)

time: 164 us -> 163 us (level)
    unnamed x25 -> x24, local copies, waits for them, and re-layouts: 5.24 us -> 5.23 us
where the time goes in v1:
time: 163 us
  blocking collectives  101 us (62%)
  waiting for transfers between devices  29.8 us (18%)
  between operations  14.9 us (9%)
  local copies, waits for them, and re-layouts  9.24 us (6%)
  other arithmetic  6.46 us (4%)
    unnamed x2, waiting for transfers between devices  29.8 us
    all_gather x1, blocking collectives, body(): chain_j = lax.all_gather(chain_own, 'row', axis=0, tiled=True)  26.8 us
    all_gather x1, blocking collectives, body(): now = lax.all_gather(my_data, 'row')  22.5 us
    all_gather x1, blocking collectives, body(): radius_j = lax.all_gather(radius_own, 'row', axis=0, tiled=True)  22.3 us
    psum x1, blocking collectives, body(): grad_all = lax.psum(pair_part[3], 'col')  12.4 us
    psum x1, blocking collectives, body(): born_all = lax.psum(born_part, 'col')  11.9 us
    all_gather x1, blocking collectives, body(): side_i = lax.all_gather(own_data, 'col', axis=1, tiled=True)  5.34 us
    unnamed x24, local copies, waits for them, and re-layouts  5.23 us
  transfers between devices with their start and end apart: 1, of which 1 were waited for; matrix products, arithmetic and copies ran while one was open for 0% of the time, Pallas kernels for 0%

profile of v1, /device:TPU:0, one launch (start us, length us, event | category | flops | bytes accessed | tf_op | source)
XLA Modules:
  0.0 162.5 jit_solution(17185935407784882806)
XLA Ops:
  7.2 1.4 maximum_bitcast_fusion
  9.3 0.7 copy-done.7
  9.9 0.7 copy-done.4
  10.8 0.6 copy-done.1
  11.4 0.7 copy-done.8
  12.1 5.3 %all_gather.15 = f32[10,512]{1,0:T(8,128)S(1)} all-gather(f32[10,256]{1,0:T(8,128)S(1)} %pad_maximum_fusion.4), channel_id=1, replica_groups=mesh['row'=16,'col'=2] {'col'}, dimensions={1}, use_global_device_ids=true | all-gather | bytes 30720 | tf_op jit(solution)/shard_map/all_gather | solution.py:155
  17.5 0.7 copy-done.6
  18.2 22.5 %all-gather.1 = f32[16,7,256]{2,1,0:T(8,128)S(1)} all-gather(f32[1,7,256]{2,1,0:T(8,128)S(1)} %slice_bitcast_fusion), channel_id=2, replica_groups=mesh['row'=16,'col'=2] {'row'}, dimensions={0}, use_global_device_ids=true | all-gather | bytes 121856 | tf_op jit(solution)/shard_map/all_gather | solution.py:157
  40.8 2.5 %while.37 = (s32[]{:T(128)}, f32[4,1,128]{2,0,1:T(4,128)S(1)}, s32[]{:T(128)}, s32[32]{0:T(128)S(1)}, f32[32]{0:T(128)S(1)}, /*index=5*/f32[32]{0:T(128)S(1)}, f...) while((s32[]{:T(128)}, f32[4,1,128]{2,0,1:T(4,128)S(1)}, ...), condition=%wide.region_5.6_spmd.clone, body=%wide.region_2.5_spmd.clone.sunk | while | flops 2036306 | bytes 881111 | solution.py:135
  40.9 0.6 gather_fusion.1
  41.6 0.6 gather_fusion
  42.2 0.3 multiply_reduce_fusion.3
  42.7 0.4 fusion.112
  43.3 11.9 %psum.14 = f32[512]{0:T(512)S(1)} all-reduce(f32[512]{0:T(512)S(1)} %bitcast.175), channel_id=1, replica_groups=mesh['row'=16,'col'=2] {'col'}, use_global_device_ids=true, to_apply=%region_6.7 | all-reduce | flops 512 | bytes 4096 | tf_op jit(solution)/shard_map/psum | solution.py:179
  55.3 22.3 %all-gather.2 = f32[16,1,256]{2,1,0:T(1,128)S(1)} all-gather(f32[1,1,256]{2,1,0:T(1,128)S(1)} %bitcast.179), channel_id=1, replica_groups=mesh['row'=16,'col'=2] {'row'}, dimensions={0}, use_global_device_ids=true | all-gather | bytes 17408 | tf_op jit(solution)/shard_map/all_gather | solution.py:182
  77.7 3.1 %while.38 = (s32[]{:T(128)}, f32[4,4,128]{2,0,1:T(4,128)S(1)}, s32[]{:T(128)}, s32[32]{0:T(128)S(1)}, f32[32]{0:T(128)S(1)}, /*index=5*/f32[32]{0:T(128)S(1)}, f...) while((s32[]{:T(128)}, f32[4,4,128]{2,0,1:T(4,128)S(1)}, ...), condition=%wide.region_11.14_spmd.clone, body=%wide.region_7.13_spmd.clone.sunk | while | flops 3619922 | bytes 1462743 | solution.py:135
  77.8 0.6 gather_fusion.3
  78.5 0.6 gather_fusion.2
  79.1 0.3 fusion.116
  79.6 0.5 fusion.120
  80.1 0.5 fusion.121
  80.8 12.4 %psum.15 = f32[512]{0:T(512)S(1)} all-reduce(f32[512]{0:T(512)S(1)} %slice_bitcast_fusion.1), channel_id=1, replica_groups=mesh['row'=16,'col'=2] {'col'}, use_global_device_ids=true, to_apply=%region_12.15 | all-reduce | flops 512 | bytes 4096 | tf_op jit(solution)/shard_map/psum | solution.py:186
  93.3 26.8 %all-gather.3 = f32[16,1,256]{2,1,0:T(1,128)S(1)} all-gather(f32[1,1,256]{2,1,0:T(1,128)S(1)} %bitcast.178), channel_id=1, replica_groups=mesh['row'=16,'col'=2] {'row'}, dimensions={0}, use_global_device_ids=true | all-gather | bytes 17408 | tf_op jit(solution)/shard_map/all_gather | solution.py:191
  120.2 3.2 %while.39 = (s32[]{:T(128)}, f32[4,3,128]{2,0,1:T(4,128)S(1)}, s32[]{:T(128)}, s32[32]{0:T(128)S(1)}, f32[32]{0:T(128)S(1)}, /*index=5*/f32[32]{0:T(128)S(1)}, f...) while((s32[]{:T(128)}, f32[4,3,128]{2,0,1:T(4,128)S(1)}, ...), condition=%wide.region_16.19_spmd.clone, body=%wide.region_13.18_spmd.clone.sunk | while | flops 4188242 | bytes 1489367 | solution.py:135
  120.3 0.6 gather_fusion.5
  121.0 0.6 gather_fusion.4
  122.1 0.6 fusion.127
  122.7 0.5 fusion.128
  123.4 0.9 copy.45
  124.3 29.8 %reduce-scatter.4.cloned.1.call-done = f32[256,3]{1,0:T(8,128)} async-done(((f32[512,3]{1,0:T(8,128)}), f32[256,3]{1,0:T(8,128)}) %reduce-scatter.4.cloned.1.call-update) | async-done | bytes 3088
  154.1 1.0 copy.44
  155.1 0.6 multiply_add_fusion
  (87 shorter events, 2.8 us)
Async XLA Ops:
  7.2 146.9 %reduce-scatter.4.cloned.1.call-start = ((), (), s32[]{:S(2)}) async-start(), calls=%async_computation.1 | async-start | bytes 393216
  9.3 0.7 copy-start.7
  9.9 0.7 copy-start.4
  10.6 0.7 copy-start.1
  10.6 0.7 copy-start.5
  10.7 0.7 copy-start
  11.4 0.7 copy-start.3
  11.4 0.7 copy-start.8
  17.5 0.7 copy-start.6
  155.1 0.6 copy-start.2
Sparse Core Ops, SparseCore 0:
  124.4 29.6 reduce-scatter.3
